TPU v7x, 32 devices: a whole 2x2x4 slice. The times are simulated.
32 devices in a mesh: rows: 8 (over z, x), grp: 4 (over y, core).
Axes of the slice: x: 2, y: 2, z: 4, core: 2. Of those that a mesh axis runs over, the one named last changes fastest.
Arguments:
- queries: bfloat16 [2048, 1024], P('rows'), may hold values from -12 to 12
- passages: bfloat16 [8192, 1024], P(('rows', 'grp')), may hold values from -12 to 12
- positive: int32 [2048], P('rows'), may hold values from 0 to 8191
Outputs:
- losses: float32 [2048], P('rows')
- grad_queries: float32 [2048, 1024], P('rows')
- grad_passages: float32 [8192, 1024], P(('rows', 'grp'))
All inputs are finite; a program needn't handle non-finite values.
Results may differ from a plain program's by a relative error of at most 0.0015.
Values may be sent and summed in bfloat16 or wider, within the bound.
A program may use at most 128 MiB of HBM per device.

v0:
```python
import math

import jax
import jax.numpy as jnp
from jax import lax
from jax.sharding import PartitionSpec as P

lowest = -1e30


def combined_all(value, axis, combine):
    everything = jax.tree.map(lambda part: lax.all_gather(part, axis), value)
    leading = jax.tree.map(lambda part: part[0], everything)

    def step(k, so_far):
        return combine(so_far, jax.tree.map(lambda part: part[k], everything))

    return lax.fori_loop(1, lax.axis_size(axis), step, leading)


def score_block(left_rows, right_rows):
    return lax.dot_general(
        left_rows, right_rows, (((1,), (1,)), ((), ())), preferred_element_type=jnp.float32
    )


def block_size(length):
    return math.gcd(length, 1024)


def combine_parts(first_part, second_part):
    left_max, left_sum, left_pos = first_part
    right_max, right_sum, right_pos = second_part
    joined = jnp.maximum(left_max, right_max)
    merged_sum = left_sum * jnp.exp(left_max - joined) + right_sum * jnp.exp(right_max - joined)
    return (joined, merged_sum, left_pos + right_pos)


def local(queries, passages, positive):
    per_dev = passages.shape[0]
    rows_q = queries.shape[0]
    width = queries.shape[1]
    groups = lax.axis_size("grp")
    group_id = lax.axis_index("grp")
    row_id = lax.axis_index("rows")
    block_id = positive // per_dev
    local_row = positive % per_dev
    share_pos = jnp.where(
        block_id % groups == group_id, block_id // groups * per_dev + local_row, -1
    )
    initial = (
        jnp.full((rows_q,), lowest, jnp.float32),
        jnp.zeros((rows_q,), jnp.float32),
        jnp.zeros((rows_q,), jnp.float32),
    )
    segment = lax.all_gather(passages, "rows", axis=0, tiled=True)
    length = segment.shape[0]
    block_rows = block_size(length)

    def forward_inner_step(block_index, state):
        running_max, running_sum, chosen = state
        first = block_index * block_rows
        sub_block = lax.dynamic_slice_in_dim(segment, first, block_rows, 0)
        scores = score_block(queries, sub_block)
        column = first + lax.iota(jnp.int32, block_rows)
        chosen = chosen + jnp.sum(
            jnp.where(share_pos[:, None] == column[None, :], scores, 0.0), axis=1
        )
        newbest = jnp.maximum(running_max, jnp.max(scores, axis=1))
        running_sum = running_sum * jnp.exp(running_max - newbest) + jnp.sum(
            jnp.exp(scores - newbest[:, None]), axis=1
        )
        return (newbest, running_sum, chosen)

    partial_state = lax.fori_loop(0, length // block_rows, forward_inner_step, initial)
    running_max, running_sum, chosen = combined_all(partial_state, "grp", combine_parts)
    log_total = running_max + jnp.log(running_sum)
    losses = log_total - chosen
    all_lse, all_positive = (
        lax.all_gather(log_total, "rows", axis=0, tiled=True),
        lax.all_gather(positive, "rows", axis=0, tiled=True),
    )
    own_base = (row_id * groups + group_id) * per_dev
    query_start = jnp.zeros((rows_q, width), jnp.float32)
    passage_start = jnp.zeros((per_dev, width), jnp.float32)
    query_segment = lax.all_gather(passages, "rows", axis=0, tiled=True)
    length = query_segment.shape[0]
    query_block_rows = block_size(length)

    def query_inner_step(block_index, accum):
        first = block_index * query_block_rows
        sub_block = lax.dynamic_slice_in_dim(query_segment, first, query_block_rows, 0)
        scores = score_block(queries, sub_block)
        weights = jnp.exp(scores - log_total[:, None]).astype(jnp.bfloat16)
        accum = accum + jnp.dot(weights, sub_block, preferred_element_type=jnp.float32)
        hit_row = share_pos - first
        inside = (hit_row >= 0) & (hit_row < query_block_rows)
        picked = jnp.take(sub_block, jnp.clip(hit_row, 0, query_block_rows - 1), axis=0).astype(
            jnp.float32
        )
        return accum - jnp.where(inside[:, None], picked, 0.0)

    query_part = lax.fori_loop(0, length // query_block_rows, query_inner_step, query_start)
    passage_segment = lax.all_gather(queries, "rows", axis=0, tiled=True)
    length = passage_segment.shape[0]
    passage_block_rows = block_size(length)

    def passage_inner_step(block_index, accum):
        first = block_index * passage_block_rows
        sub_block = lax.dynamic_slice_in_dim(passage_segment, first, passage_block_rows, 0)
        block_lse = lax.dynamic_slice_in_dim(all_lse, first, passage_block_rows, 0)
        block_pos = lax.dynamic_slice_in_dim(all_positive, first, passage_block_rows, 0)
        scores = score_block(sub_block, passages)
        weights = jnp.exp(scores - block_lse[:, None]).astype(jnp.bfloat16)
        accum = accum + lax.dot_general(
            weights, sub_block, (((0,), (0,)), ((), ())), preferred_element_type=jnp.float32
        )
        hit_row = block_pos - own_base
        inside = (hit_row >= 0) & (hit_row < per_dev)
        target_slot = jnp.where(inside, hit_row, per_dev).astype(jnp.int32)
        return accum.at[target_slot].add(-sub_block.astype(jnp.float32), mode="drop")

    grad_passages = lax.fori_loop(
        0, length // passage_block_rows, passage_inner_step, passage_start
    )
    grad_queries = lax.psum(query_part, "grp")
    return (losses, grad_queries, grad_passages)


def solution(mesh):
    placed = (P("rows", None), P(("rows", "grp"), None), P("rows"))
    return jax.shard_map(
        local,
        mesh=mesh,
        in_specs=placed,
        out_specs=(P("rows"), P("rows", None), P(("rows", "grp"), None)),
        check_vma=False,
    )
```

profile of v0, /device:TPU:0, one launch (start us, length us, event | category | flops | bytes accessed | tf_op | source)
XLA Modules:
  0.0 205.9 jit_solution(9051152842983273192)
XLA Ops:
  7.2 0.0 all-gather.11.cloned.1.call-start
  7.2 0.7 all-gather.11.cloned.1.call-update
  7.9 0.0 all-gather.13.cloned.1.call-start
  7.9 0.7 all-gather.13.cloned.1.call-update
  8.6 0.0 all-reduce.2.cloned.1.call-start
  8.7 22.8 %all-gather.7 = s32[8,1,256]{2,1,0:T(1,128)S(1)} all-gather(s32[1,1,256]{2,1,0:T(1,128)} %bitcast.77), channel_id=1, replica_groups=mesh['rows'=8,'grp'=4] {'rows'}, dimensions={0}, use_global_device_ids=true | all-gather | bytes 9216 | tf_op jit(solution)/shard_map/all_gather | solution.py:81
  31.6 0.7 compare_select_fusion.3
  32.3 53.4 %all-gather.11.cloned.1.call-done = bf16[2048,1024]{1,0:T(8,128)(2,1)} async-done(((bf16[256,1024]{1,0:T(8,128)(2,1)}), bf16[2048,1024]{1,0:T(8,128)(2,1)}) %all-gather.11.cloned.1.call-update) | async-done | bytes 4194320 | tf_op jit(solution)/shard_map/all_gather | solution.py:56
  85.7 5.5 %while.66 = (s32[]{:T(128)}, f32[256]{0:T(256)S(1)}, f32[256]{0:T(256)S(1)}, f32[256]{0:T(256)S(1)}, bf16[2048,1024]{1,0:T(8,128)(2,1)}, /*index=5*/bf16[256,102...) while((s32[]{:T(128)}, f32[256]{0:T(256)S(1)}, ...), condition=%wide.region_4.5_spmd.clone, body=%wide.region_0.4_spmd.clone.sunk | while | flops 538446336 | bytes 4745398 | solution.py:75
  85.7 2.4 %fusion.64 = (f32[256]{0:T(256)S(1)}, f32[1024,256]{1,0:T(8,128)S(1)}) fusion(bf16[256,1024]{1,0:T(8,128)(2,1)} %get-tuple-element.881, bf16[2048,1024]{1,0:T(8,128)(2,1)} %get-tuple-element.880, s32[]{:T(128)S(6)} %select_n.172), kind=kOutput, calls=%fused_computation.66.clone.1 | convolution fusion | flops 537132800 | bytes 3671044 | tf_op jit(solution)/shard_map/while/body/eval_jaxpr/dot_general | solution.py:22
  88.1 0.3 fusion.66
  88.4 2.4 %fusion.64 = (f32[256]{0:T(256)S(1)}, f32[1024,256]{1,0:T(8,128)S(1)}) fusion(bf16[256,1024]{1,0:T(8,128)(2,1)} %get-tuple-element.881, bf16[2048,1024]{1,0:T(8,128)(2,1)} %get-tuple-element.880, s32[]{:T(128)S(6)} %select_n.172), kind=kOutput, calls=%fused_computation.66.clone.1 | convolution fusion | flops 537132800 | bytes 3671044 | tf_op jit(solution)/shard_map/while/body/eval_jaxpr/dot_general | solution.py:22
  90.9 0.3 fusion.66
  91.2 5.1 %all-gather.3 = f32[4,1,256]{2,1,0:T(1,128)S(1)} all-gather(f32[1,1,256]{2,1,0:T(1,128)S(1)} %bitcast.60), channel_id=2, replica_groups=mesh['rows'=8,'grp'=4] {'grp'}, dimensions={0}, use_global_device_ids=true | all-gather | bytes 5120 | tf_op jit(solution)/shard_map/all_gather | solution.py:12
  96.3 5.1 %all-gather.4 = f32[4,1,256]{2,1,0:T(1,128)S(1)} all-gather(f32[1,1,256]{2,1,0:T(1,128)S(1)} %bitcast.71), channel_id=3, replica_groups=mesh['rows'=8,'grp'=4] {'grp'}, dimensions={0}, use_global_device_ids=true | all-gather | bytes 5120 | tf_op jit(solution)/shard_map/all_gather | solution.py:12
  101.3 5.1 %all-gather.5 = f32[4,1,256]{2,1,0:T(1,128)S(1)} all-gather(f32[1,1,256]{2,1,0:T(1,128)S(1)} %bitcast.72), channel_id=4, replica_groups=mesh['rows'=8,'grp'=4] {'grp'}, dimensions={0}, use_global_device_ids=true | all-gather | bytes 5120 | tf_op jit(solution)/shard_map/all_gather | solution.py:12
  106.4 0.2 while.64
  106.6 0.6 fusion.38
  107.2 18.4 %all-gather.6 = f32[8,1,256]{2,1,0:T(1,128)S(1)} all-gather(f32[1,1,256]{2,1,0:T(1,128)S(1)} %bitcast.76), channel_id=1, replica_groups=mesh['rows'=8,'grp'=4] {'rows'}, dimensions={0}, use_global_device_ids=true | all-gather | bytes 9216 | tf_op jit(solution)/shard_map/all_gather | solution.py:80
  125.6 13.9 %while.67 = (s32[]{:T(128)}, f32[256,1024]{1,0:T(8,128)}, bf16[2048,1024]{1,0:T(8,128)(2,1)}, bf16[256,1024]{1,0:T(8,128)(2,1)}, f32[256]{0:T(256)S(1)}, /*index...) while((s32[]{:T(128)}, f32[256,1024]{1,0:T(8,128)}, ...), condition=%wide.region_8.9_spmd.clone, body=%wide.region_7.8_spmd.clone.sunk | while | flops 1075843584 | bytes 12595401 | solution.py:103
  125.6 0.0 copy-start.1
  125.6 1.8 constant_dynamic-slice_fusion.9
  127.5 1.2 gather_fusion
  128.6 0.0 copy-done.1
  128.7 3.3 %fusion.70 = f32[256,1024]{1,0:T(8,128)} fusion(bf16[1024,1024]{1,0:T(8,128)(2,1)S(1)} %constant_dynamic-slice_fusion.9, f32[256,1024]{1,0:T(8,128)} %get-tuple-element.928, bf16[256,1024]{1,0:T(8,128)(2,1)S(1)} %copy-done.1, bf16[256,1024]{1,0:T(8,128)(2,1)S(1)} %gather_fusion, f32[256]{0:T(256)S(1)} %get-tuple-element.941, ...), kind=kOutput, calls=%fused_computation.37.clone.1 | convolution fusion | flops 1075838976 | bytes 5244417 | tf_op jit(solution)/shard_map/while/body/eval_jaxpr/dot_general | solution.py:95
  131.9 0.0 copy-start.1
  132.0 1.8 constant_dynamic-slice_fusion.9
  133.8 1.2 gather_fusion
  135.0 0.0 copy-done.1
  135.0 4.5 %fusion.70 = f32[256,1024]{1,0:T(8,128)} fusion(bf16[1024,1024]{1,0:T(8,128)(2,1)S(1)} %constant_dynamic-slice_fusion.9, f32[256,1024]{1,0:T(8,128)} %get-tuple-element.928, bf16[256,1024]{1,0:T(8,128)(2,1)S(1)} %copy-done.1, bf16[256,1024]{1,0:T(8,128)(2,1)S(1)} %gather_fusion, f32[256]{0:T(256)S(1)} %get-tuple-element.941, ...), kind=kOutput, calls=%fused_computation.37.clone.1 | convolution fusion | flops 1075838976 | bytes 5244417 | tf_op jit(solution)/shard_map/while/body/eval_jaxpr/dot_general | solution.py:95
  139.5 0.0 all-reduce.2.cloned.1.call-update
  139.5 19.6 %all-gather.13.cloned.1.call-done = bf16[2048,1024]{1,0:T(8,128)(2,1)} async-done(((bf16[256,1024]{1,0:T(8,128)(2,1)}), bf16[2048,1024]{1,0:T(8,128)(2,1)}) %all-gather.13.cloned.1.call-update) | async-done | bytes 4194320 | tf_op jit(solution)/shard_map/all_gather | solution.py:104
  159.2 0.1 broadcast.167
  159.3 29.8 %while.65 = (s32[]{:T(128)}, f32[256,1024]{1,0:T(8,128)S(1)}, bf16[2048,1024]{1,0:T(8,128)(2,1)}, bf16[256,1024]{1,0:T(8,128)(2,1)}, f32[2048]{0:T(1024)S(1)}, /...) while((s32[]{:T(128)}, f32[256,1024]{1,0:T(8,128)S(1)}, ...), condition=%wide.region_12.13_spmd, body=%wide.region_10.12_spmd.sunk | while | flops 1077682176 | bytes 9983667 | solution.py:123
  159.3 4.7 %fusion.62 = f32[256,1024]{1,0:T(8,128)S(1)} fusion(f32[256,1024]{1,0:T(8,128)S(1)} %get-tuple-element.959, bf16[2048,1024]{1,0:T(8,128)(2,1)} %get-tuple-element.971, s32[]{:T(128)S(6)} %select_n.170, bf16[256,1024]{1,0:T(8,128)(2,1)} %get-tuple-element.972, f32[1024]{0:T(1024)S(1)} %dynamic_slice.111), kind=kOutput, calls=%fused_computation.16.clone.1 | convolution fusion | flops 1074528256 | bytes 6820864 | tf_op jit(solution)/shard_map/while/body/eval_jaxpr/dot_general | solution.py:115
  164.1 10.1 %scatter_custom_fusion.5 = f32[256,1024]{1,0:T(8,128)S(1)} fusion(f32[256,1024]{1,0:T(8,128)S(1)} %fusion.62, s32[1024]{0:T(1024)S(1)} %compare_select_fusion.6, bf16[2048,1024]{1,0:T(8,128)(2,1)} %get-tuple-element.971, s32[]{:T(128)S(6)} %select_n.170, s32[]{:T(128)} %constant.224.clone.1..sunk.1), kind=kCustom, calls=%fused_computation.6.clone.1 | custom fusion | flops 3145728 | bytes 3146244 | tf_op jit(solution)/shard_map/while/body/eval_jaxpr/scatter-add | solution.py:121
  174.2 4.7 %fusion.62 = f32[256,1024]{1,0:T(8,128)S(1)} fusion(f32[256,1024]{1,0:T(8,128)S(1)} %get-tuple-element.959, bf16[2048,1024]{1,0:T(8,128)(2,1)} %get-tuple-element.971, s32[]{:T(128)S(6)} %select_n.170, bf16[256,1024]{1,0:T(8,128)(2,1)} %get-tuple-element.972, f32[1024]{0:T(1024)S(1)} %dynamic_slice.111), kind=kOutput, calls=%fused_computation.16.clone.1 | convolution fusion | flops 1074528256 | bytes 6820864 | tf_op jit(solution)/shard_map/while/body/eval_jaxpr/dot_general | solution.py:115
  179.0 10.1 %scatter_custom_fusion.5 = f32[256,1024]{1,0:T(8,128)S(1)} fusion(f32[256,1024]{1,0:T(8,128)S(1)} %fusion.62, s32[1024]{0:T(1024)S(1)} %compare_select_fusion.6, bf16[2048,1024]{1,0:T(8,128)(2,1)} %get-tuple-element.971, s32[]{:T(128)S(6)} %select_n.170, s32[]{:T(128)} %constant.224.clone.1..sunk.1), kind=kCustom, calls=%fused_computation.6.clone.1 | custom fusion | flops 3145728 | bytes 3146244 | tf_op jit(solution)/shard_map/while/body/eval_jaxpr/scatter-add | solution.py:121
  189.1 0.0 copy-start
  189.1 7.9 %all-reduce.2.cloned.1.call-done = f32[256,1024]{1,0:T(8,128)} async-done(((f32[256,1024]{1,0:T(8,128)}), f32[256,1024]{1,0:T(8,128)}) %all-reduce.2.cloned.1.call-update) | async-done | bytes 1048592 | tf_op jit(solution)/shard_map/psum | solution.py:126
  197.0 2.3 %copy.53 = f32[256,1024]{1,0:T(8,128)} copy(f32[256,1024]{1,0:T(8,128)} %all-reduce.2.cloned.1.call-done) | data formatting | bytes 2097152
  199.3 0.0 copy-done
  (40 shorter events, 0.3 us)
Async XLA Ops:
  7.2 78.5 %all-gather.11.cloned.1.call-start = ((), (), s32[]{:S(2)}) async-start(), calls=%async_computation | async-start | bytes 4718592 | tf_op jit(solution)/shard_map/all_gather | solution.py:56
  7.9 151.3 %all-gather.13.cloned.1.call-start = ((), (), s32[]{:S(2)}) async-start(), calls=%async_computation.2 | async-start | bytes 4718592 | tf_op jit(solution)/shard_map/all_gather | solution.py:104
  8.6 188.4 %all-reduce.2.cloned.1.call-start = ((), (), s32[]{:S(2)}) async-start(), calls=%async_computation.1 | async-start | bytes 2097152 | tf_op jit(solution)/shard_map/psum | solution.py:126
  125.6 3.1 %copy-start.1 = (bf16[256,1024]{1,0:T(8,128)(2,1)S(1)}, bf16[256,1024]{1,0:T(8,128)(2,1)}, u32[]{:S(2)}) copy-start(bf16[256,1024]{1,0:T(8,128)(2,1)} %get-tuple-element.940) | copy-start | bytes 1572868 | tf_op jit(solution)/shard_map/while
  131.9 3.0 %copy-start.1 = (bf16[256,1024]{1,0:T(8,128)(2,1)S(1)}, bf16[256,1024]{1,0:T(8,128)(2,1)}, u32[]{:S(2)}) copy-start(bf16[256,1024]{1,0:T(8,128)(2,1)} %get-tuple-element.940) | copy-start | bytes 1572868 | tf_op jit(solution)/shard_map/while
  189.1 10.2 %copy-start = (f32[256,1024]{1,0:T(8,128)}, f32[256,1024]{1,0:T(8,128)S(1)}, u32[]{:S(2)}) copy-start(f32[256,1024]{1,0:T(8,128)S(1)} %get-tuple-element.982) | copy-start | bytes 3145732
Sparse Core Ops, SparseCore 0:
  10.1 75.5 all-gather.10
  87.8 71.3 all-gather.12
  162.1 34.8 all-reduce.1
where the time goes:
time: 206 us
  waiting for transfers between devices  82.3 us (40%)
  blocking collectives  56.4 us (27%)
  other arithmetic  22.2 us (11%)
  matrix products  22.1 us (11%)
  between operations  13.8 us (7%)
  local copies, waits for them, and re-layouts  8.5 us (4%)
    all_gather x1, waiting for transfers between devices, local(): segment = lax.all_gather(passages, 'rows', axis=0, tiled=True)  53.4 us
    all_gather x1, blocking collectives, local(): lax.all_gather(positive, 'rows', axis=0, tiled=True)  22.8 us
    scatter-add x2, other arithmetic, passage_inner_step(): accum.at[target_slot].add(-sub_block.astype(jnp.float32), mode='drop')  20.2 us
    all_gather x1, waiting for transfers between devices, local(): passage_segment = lax.all_gather(queries, 'rows', axis=0, tiled=True)  19.6 us
    all_gather x1, blocking collectives, local(): lax.all_gather(log_total, 'rows', axis=0, tiled=True)  18.4 us
    all_gather x3, blocking collectives, combined_all(): everything = jax.tree.map(lambda part: lax.all_gather(part, axis), value)  15.2 us
    dot_general x2, matrix products, passage_inner_step(): lax.dot_general(weights, sub_block, (((0,), (0,)), ((), ())), preferred_e...  9.45 us
    psum x1, waiting for transfers between devices, local(): grad_queries = lax.psum(query_part, 'grp')  7.93 us
  transfers between devices with their start and end apart: 3, of which 3 were waited for; matrix products, arithmetic and copies ran while one was open for 25% of the time, Pallas kernels for 0%

commit v1 on v0

v1 whole, which is shorter than its diff:
```python
import functools

import jax
import jax.numpy as jnp
from jax import lax
from jax.experimental import pallas as pl
from jax.experimental.pallas import tpu as pltpu
from jax.sharding import PartitionSpec as P

lowest = -1e30
MESH = pl.DeviceIdType.MESH
F32 = jnp.float32
BF16 = jnp.bfloat16


def dot_nt(a, b):
    return lax.dot_general(a, b, (((1,), (1,)), ((), ())), preferred_element_type=F32)


def dot_nn(a, b):
    return jnp.dot(a, b, preferred_element_type=F32)


def kernel(
    R, G, q_hbm, p_hbm, pos_col_ref, pos_row_ref,
    loss_ref, gq_ref, gp_ref,
    p_all, q_all, pos_all, lse_all, stats, stats_in, lse_buf,
    acc, hit_acc, m_ref, l_ref, c_ref, s_keep, w_keep,
    got_core, half_sum, got_y, done_half, got_half,
    local_sem, p_send, p_recv, q_send, q_recv, f_send, f_recv,
    pos_send, pos_recv, lse_send, lse_recv, st_send, st_recv,
    x_send, x_recv, y_send, y_recv,
):
    r = lax.axis_index("rows")
    g = lax.axis_index("grp")
    half_ring = R // 2
    _, Pd, D = p_all.shape
    Rq = q_all.shape[1]
    tile = min(256, D)
    z, x = r // 2, r % 2
    place = z + x * (R - 1 - 2 * z)

    def row_of(where):
        far = where // half_ring
        return 2 * (where + far * (R - 1 - 2 * where)) + far

    def origin(way, d):
        return row_of((place + (2 * way - 1) * d + R) % R)

    right, left = row_of((place + 1) % R), row_of((place + R - 1) % R)
    target = (right, left)
    core = g % 2
    partner = g + 1 - 2 * core

    def to_row(row):
        return (row, g)

    def to_grp(col):
        return (r, col)

    def remote(src, dst, send, recv, device):
        return pltpu.make_async_remote_copy(
            src_ref=src, dst_ref=dst, send_sem=send, recv_sem=recv,
            device_id=device, device_id_type=MESH,
        )

    load_p = pltpu.make_async_copy(p_hbm, p_all.at[r], local_sem.at[0])
    load_q = pltpu.make_async_copy(q_hbm, q_all.at[r], local_sem.at[1])
    load_p.start()
    load_q.start()

    barrier = pltpu.get_barrier_semaphore()
    for k in range(1, R):
        pl.semaphore_signal(barrier, inc=1, device_id=to_row((r + k) % R), device_id_type=MESH)
    for k in range(1, G):
        pl.semaphore_signal(barrier, inc=1, device_id=to_grp((g + k) % G), device_id_type=MESH)
    pl.semaphore_wait(barrier, R - 1 + G - 1)

    pc = Pd // 2

    def p_copy(way, src, d, chunk):
        piece = p_all.at[src, pl.ds(chunk * pc, pc)]
        return remote(piece, piece, p_send.at[way, d, chunk], p_recv.at[way, d, chunk],
                      to_row(target[way]))

    qc = Rq // 4

    def q_copy(way, src, d, chunk):
        piece = q_all.at[src, pl.ds(pl.multiple_of(core * (2 * qc) + chunk * qc, qc), qc)]
        return remote(piece, piece, q_send.at[way, d, chunk], q_recv.at[way, d, chunk],
                      to_row(target[way]))

    def f_copy(way, src, d, chunk, whose):
        piece = q_all.at[src, pl.ds(pl.multiple_of(whose * (2 * qc) + chunk * qc, qc), qc)]
        return remote(piece, piece, f_send.at[way, d, chunk], f_recv.at[way, d, chunk],
                      to_grp(partner))

    load_p.wait()
    for chunk in range(2):
        for way in range(2):
            p_copy(way, r, 1, chunk).start()
    load_q.wait()

    def pos_copy(k, src):
        return remote(pos_row_ref, pos_all.at[src], pos_send.at[k], pos_recv.at[k],
                      to_row((r + k) % R))

    for k in range(1, R):
        pos_copy(k, r).start()
    pos_all[r] = pos_row_ref[...]

    m_ref[...] = jnp.full((Rq, 1), lowest, F32)
    l_ref[...] = jnp.zeros((Rq, 1), F32)
    c_ref[...] = jnp.zeros((Rq, 1), F32)
    acc[...] = jnp.zeros((Rq, D), F32)
    hit_acc[...] = jnp.zeros((Rq, D), F32)

    def use_passages(u):
        block = p_all.at[u]
        s = dot_nt(q_all[r], block[...])
        column = (u * G + g) * Pd + lax.broadcasted_iota(jnp.int32, (Rq, Pd), 1)
        hit = pos_col_ref[...] == column
        c_ref[...] += jnp.sum(jnp.where(hit, s, 0.0), axis=1, keepdims=True)
        old = m_ref[...]
        new = jnp.maximum(old, jnp.max(s, axis=1, keepdims=True))
        scale = jnp.exp(old - new)
        w = jnp.exp(s - new)
        l_ref[...] = l_ref[...] * scale + jnp.sum(w, axis=1, keepdims=True)
        m_ref[...] = new
        w = w.astype(BF16)
        one = jnp.where(hit, 1.0, 0.0).astype(BF16)
        for t in range(0, D, tile):
            cols = pl.ds(t, tile)
            acc[:, cols] = acc[:, cols] * scale + dot_nn(w, block[:, cols])
            hit_acc[:, cols] += dot_nn(one, block[:, cols])

    use_passages(r)

    def p_step(d, carry):
        for chunk in range(2):
            for way in range(2):
                src = origin(way, d)
                p_copy(way, src, d, chunk).wait_recv()
                if chunk == way:
                    p_copy(way, src, d + 1, chunk).start()
                else:
                    @pl.when(d + 1 < half_ring)
                    def _():
                        p_copy(way, src, d + 1, chunk).start()

        @pl.when(d + 1 == half_ring)
        def _():
            for chunk in range(2):
                for way in range(2):
                    q_copy(way, r, 1, chunk).start()

        for way in range(2):
            use_passages(origin(way, d))
        return carry

    lax.fori_loop(1, half_ring, p_step, 0)
    last = origin(0, half_ring)
    for way in range(2):
        p_copy(way, last, half_ring, way).wait_recv()
    use_passages(last)

    lane = lax.broadcasted_iota(jnp.int32, (Rq, 128), 1)
    cols = jnp.where(lane == 0, m_ref[...], jnp.where(lane == 1, l_ref[...], c_ref[...]))
    stats[...] = cols.T[0:8, :]

    def st_copy(k, src):
        return remote(stats, stats_in.at[src], st_send.at[k], st_recv.at[k],
                      to_grp((g + k) % G))

    for k in range(1, G):
        st_copy(k, g).start()
    for k in range(1, G):
        st_copy(k, (g - k + G) % G).wait_recv()
    stats_in[g] = stats[...]
    parts = [stats_in[k] for k in range(G)]
    top = functools.reduce(jnp.maximum, [v[0:1] for v in parts])
    total = functools.reduce(jnp.add, [v[1:2] * jnp.exp(v[0:1] - top) for v in parts])
    lse = top + jnp.log(total)
    loss_ref[...] = lse - functools.reduce(jnp.add, [v[2:3] for v in parts])
    lse_buf[...] = jnp.broadcast_to(lse, (8, Rq))

    def lse_copy(k, src):
        return remote(lse_buf, lse_all.at[src], lse_send.at[k], lse_recv.at[k],
                      to_row((r + k) % R))

    for k in range(1, R):
        lse_copy(k, r).start()
    lse_all[r] = lse_buf[...]

    lse_col = jnp.broadcast_to(lse, (128, Rq)).T[:, 0:1]
    hr = Rq // 2
    final = jnp.exp(m_ref[...] - lse_col)
    acc[...] = acc[...] * final - hit_acc[...]
    mine = pl.ds(pl.multiple_of(core * hr, hr), hr)
    other = pl.ds(pl.multiple_of((1 - core) * hr, hr), hr)
    core_copy = remote(acc.at[other], got_core, x_send.at[0], x_recv.at[0], to_grp(partner))
    core_copy.start()
    core_copy.wait_recv()
    half_sum[...] = acc[mine] + got_core[...]

    def y_copy(k):
        return remote(half_sum, got_y.at[k - 1], y_send.at[k], y_recv.at[k],
                      to_grp((g + 2 * k) % G))

    for k in range(1, G // 2):
        y_copy(k).start()

    gp_ref[...] = jnp.zeros((Pd, D), F32)
    base = (r * G + g) * Pd

    def use_queries(u):
        block = q_all.at[u]
        s_keep[u] = dot_nt(p_all[r], block[...])
        row = base + lax.broadcasted_iota(jnp.int32, (Pd, Rq), 0)
        one = jnp.where(row == pos_all[u][0:1], 1.0, 0.0).astype(BF16)
        for t in range(0, D, tile):
            c = pl.ds(t, tile)
            gp_ref[:, c] -= dot_nn(one, block[:, c])

    for k in range(1, R):
        pos_copy(k, (r - k + R) % R).wait_recv()
    use_queries(r)

    def q_step(d, carry):
        for chunk in range(2):
            for way in range(2):
                src = origin(way, d)
                q_copy(way, src, d, chunk).wait_recv()
                if chunk == way:
                    q_copy(way, src, d + 1, chunk).start()
                else:
                    @pl.when(d + 1 < half_ring)
                    def _():
                        q_copy(way, src, d + 1, chunk).start()
                f_copy(way, src, d, chunk, core).start()
        for way in range(2):
            src = origin(way, d)
            for chunk in range(2):
                f_copy(way, src, d, chunk, 1 - core).wait_recv()
            use_queries(src)
        return carry

    lax.fori_loop(1, half_ring, q_step, 0)
    for way in range(2):
        q_copy(way, last, half_ring, way).wait_recv()
        f_copy(way, last, half_ring, way, core).start()

    for k in range(1, G // 2):
        y_copy(k).wait_recv()
    whole = half_sum[...]
    for k in range(1, G // 2):
        whole = whole + got_y[k - 1]
    done_half[...] = whole
    back_copy = remote(done_half, got_half, x_send.at[1], x_recv.at[1], to_grp(partner))
    back_copy.start()
    gq_ref[mine] = whole

    for way in range(2):
        f_copy(way, last, half_ring, way, 1 - core).wait_recv()
    use_queries(last)
    for k in range(1, R):
        lse_copy(k, (r - k + R) % R).wait_recv()

    def weigh(u, carry):
        at = pl.ds(pl.multiple_of(u * Rq, Rq), Rq)
        w_keep[:, at] = jnp.exp(s_keep[u] - lse_all[u][0:1]).astype(BF16)
        return carry

    lax.fori_loop(0, R, weigh, 0)

    def passages_tile(t, carry):
        c = pl.ds(pl.multiple_of(t * tile, tile), tile)
        q_cols = q_all[:, :, c].reshape(R * Rq, tile)
        gp_ref[:, c] += dot_nn(w_keep[...], q_cols)
        return carry

    lax.fori_loop(0, D // tile, passages_tile, 0)

    back_copy.wait_recv()
    gq_ref[other] = got_half[...]

    def drain(d, carry):
        for chunk in range(2):
            for way in range(2):
                src = origin(way, d)

                def settle():
                    p_copy(way, src, d, chunk).wait_send()
                    q_copy(way, src, d, chunk).wait_send()
                    f_copy(way, src, d, chunk, core).wait_send()

                if chunk == way:
                    settle()
                else:
                    pl.when(d < half_ring)(settle)
        return carry

    lax.fori_loop(1, half_ring + 1, drain, 0)
    for k in range(1, R):
        pos_copy(k, r).wait_send()
        lse_copy(k, r).wait_send()
    for k in range(1, G):
        st_copy(k, g).wait_send()
    for k in range(1, G // 2):
        y_copy(k).wait_send()
    core_copy.wait_send()
    back_copy.wait_send()


def local(R, G, queries, passages, positive):
    Rq, D = queries.shape
    Pd = passages.shape[0]
    pos_col = positive[:, None]
    pos_row = jnp.broadcast_to(positive[None, :], (8, Rq))
    ring = (2, R // 2 + 1, 2)
    sem = pltpu.SemaphoreType.DMA
    vmem = pltpu.VMEM
    losses, gq, gp = pl.pallas_call(
        functools.partial(kernel, R, G),
        out_shape=(
            jax.ShapeDtypeStruct((1, Rq), F32),
            jax.ShapeDtypeStruct((Rq, D), F32),
            jax.ShapeDtypeStruct((Pd, D), F32),
        ),
        in_specs=[
            pl.BlockSpec(memory_space=pl.ANY),
            pl.BlockSpec(memory_space=pl.ANY),
            pl.BlockSpec(memory_space=vmem),
            pl.BlockSpec(memory_space=vmem),
        ],
        out_specs=[pl.BlockSpec(memory_space=vmem)] * 3,
        scratch_shapes=[
            vmem((R, Pd, D), BF16),
            vmem((R, Rq, D), BF16),
            vmem((R, 8, Rq), jnp.int32),
            vmem((R, 8, Rq), F32),
            vmem((8, Rq), F32),
            vmem((G, 8, Rq), F32),
            vmem((8, Rq), F32),
            vmem((Rq, D), F32),
            vmem((Rq, D), F32),
            vmem((Rq, 1), F32),
            vmem((Rq, 1), F32),
            vmem((Rq, 1), F32),
            vmem((R, Pd, Rq), F32),
            vmem((Pd, R * Rq), BF16),
            vmem((Rq // 2, D), F32),
            vmem((Rq // 2, D), F32),
            vmem((G // 2 - 1, Rq // 2, D), F32),
            vmem((Rq // 2, D), F32),
            vmem((Rq // 2, D), F32),
            sem((2,)),
            sem(ring), sem(ring), sem(ring), sem(ring), sem(ring), sem(ring),
            sem((R,)), sem((R,)), sem((R,)), sem((R,)), sem((G,)), sem((G,)),
            sem((2,)), sem((2,)), sem((G // 2,)), sem((G // 2,)),
        ],
        compiler_params=pltpu.CompilerParams(
            collective_id=0, has_side_effects=True, vmem_limit_bytes=60 * 1024 * 1024
        ),
        name="infonce",
    )(queries, passages, pos_col, pos_row)
    return losses[0], gq, gp


def solution(mesh):
    R, G = mesh.shape["rows"], mesh.shape["grp"]
    return jax.shard_map(
        functools.partial(local, R, G),
        mesh=mesh,
        in_specs=(P("rows", None), P(("rows", "grp"), None), P("rows")),
        out_specs=(P("rows"), P("rows", None), P(("rows", "grp"), None)),
        check_vma=False,
    )
```

time: 206 us -> 91.2 us (0.44)
  Pallas kernels: 0 us -> 82.9 us
  waiting for transfers between devices: 82.3 us -> 0 us
  blocking collectives: 56.4 us -> 0 us
  other arithmetic: 22.2 us -> 0 us
  matrix products: 22.1 us -> 0 us
  between operations: 13.8 us -> 0.66 us
    pallas_call x0 -> x1, Pallas kernels: none -> 82.9 us  [local(): pl.pallas_call(functools.partial(kernel, R, G), out_shape=(jax.ShapeDtype...]
    all_gather x2 -> x0, waiting for transfers between devices: 73 us -> none  [the longest x1 53.4 us: local(): segment = lax.all_gather(passages, 'rows', axis=0, tiled=True)]
    all_gather x5 -> x0, blocking collectives: 56.4 us -> none  [the longest x1 22.8 us: local(): lax.all_gather(positive, 'rows', axis=0, tiled=True)]
    dot_general x6 -> x0, matrix products: 22.1 us -> none  [the longest x2 9.45 us: passage_inner_step(): lax.dot_general(weights, sub_block, (((0,), (0,)), ((), ())), preferred_e...]
    scatter-add x2 -> x0, other arithmetic: 20.2 us -> none  [passage_inner_step(): accum.at[target_slot].add(-sub_block.astype(jnp.float32), mode='drop')]
    psum x1 -> x0, waiting for transfers between devices: 7.93 us -> none  [local(): grad_queries = lax.psum(query_part, 'grp')]
    dynamic_slice x10 -> x0, local copies, waits for them, and re-layouts: 3.72 us -> none  [the longest x2 3.65 us: query_inner_step(): lax.dynamic_slice_in_dim(query_segment, first, query_block_rows, 0)]
    unnamed x6 -> x9, local copies, waits for them, and re-layouts: 2.32 us -> 5.25 us
  transfers between devices with their start and end apart: 3 -> 0, of which waited for: 3 -> 0; matrix products, arithmetic and copies ran while one was open for 25% -> 0% of each run, Pallas kernels for 0% -> 0%
where the time goes in v1:
time: 91.2 us; the launch traced here: 90.2 us
  Pallas kernels  82.9 us (91%)
  local copies, waits for them, and re-layouts  6.65 us (7%)
    pallas_call x1, Pallas kernels, local(): pl.pallas_call(functools.partial(kernel, R, G), out_shape=(jax.ShapeDtype...  82.9 us
    unnamed x9, local copies, waits for them, and re-layouts  5.25 us

profile of v1, /device:TPU:0, one launch (start us, length us, event | category | flops | bytes accessed | tf_op | source)
XLA Modules:
  0.0 90.2 jit_solution(4109373060798007880)
XLA Ops:
  0.6 0.0 copy-start.1
  0.6 0.7 copy-done.1
  1.3 0.6 broadcast_in_dim.10.pos_row_ref
  1.9 0.8 copy.6.pos_col_ref
  2.7 82.9 %infonce.1 = (f32[1,256]{1,0:T(1,128)}, f32[256,1024]{1,0:T(8,128)}, f32[256,1024]{1,0:T(8,128)}) custom-call(bf16[256,1024]{1,0:T(8,128)(2,1)} %q_hbm.1, bf16[256,1024]{1,0:T(8,128)(2,1)} %p_hbm.1, s32[256,1]{1,0:T(8,128)} %copy.6.pos_col_ref, s32[8,256]{1,0:T(8,128)} %broadcast_in_dim.10.pos_row_ref), custom_call_target="tpu_custom_call" | custom-call | tf_op jit(solution)/shard_map/infonce/pallas_call | solution.py:323
  85.6 0.0 copy-start.2
  85.6 0.6 copy-done.2
  86.3 0.6 copy.10
  86.9 0.0 copy-start
  86.9 2.4 %copy.11 = f32[256,1024]{1,0:T(8,128)} copy(f32[256,1024]{1,0:T(8,128)} %get-tuple-element.13) | data formatting | bytes 2097152
  89.2 0.0 copy-done
  89.3 1.0 %copy.12 = f32[256,1024]{1,0:T(8,128)} copy(f32[256,1024]{1,0:T(8,128)S(1)} %copy-done) | data formatting | bytes 2097152
Async XLA Ops:
  0.6 0.7 copy-start.1
  85.6 0.7 copy-start.2
  86.9 2.4 %copy-start = (f32[256,1024]{1,0:T(8,128)S(1)}, f32[256,1024]{1,0:T(8,128)}, u32[]{:S(2)}) copy-start(f32[256,1024]{1,0:T(8,128)} %get-tuple-element.14) | copy-start | bytes 3145732

commit v2 on v1

--- a/solution.py
+++ b/solution.py
@@ -22,10 +22,10 @@
 
 
 def kernel(
-    R, G, q_hbm, p_hbm, pos_col_ref, pos_row_ref,
+    R, G, q_hbm, p_hbm, pos_ref,
     loss_ref, gq_ref, gp_ref,
     p_all, q_all, pos_all, lse_all, stats, stats_in, lse_buf,
-    acc, hit_acc, m_ref, l_ref, c_ref, s_keep, w_keep,
+    acc, hit_acc, m_ref, l_ref, c_ref, pos_col_ref, pos_row_ref,
     got_core, half_sum, got_y, done_half, got_half,
     local_sem, p_send, p_recv, q_send, q_recv, f_send, f_recv,
     pos_send, pos_recv, lse_send, lse_recv, st_send, st_recv,
@@ -105,6 +105,8 @@
         return remote(pos_row_ref, pos_all.at[src], pos_send.at[k], pos_recv.at[k],
                       to_row((r + k) % R))
 
+    pos_row_ref[...] = jnp.broadcast_to(pos_ref[...], (8, Rq))
+    pos_col_ref[...] = jnp.broadcast_to(pos_ref[...], (128, Rq)).T[:, 0:1]
     for k in range(1, R):
         pos_copy(k, r).start()
     pos_all[r] = pos_row_ref[...]
@@ -134,36 +136,59 @@
             acc[:, cols] = acc[:, cols] * scale + dot_nn(w, block[:, cols])
             hit_acc[:, cols] += dot_nn(one, block[:, cols])
 
+    slots = 2 * (half_ring - 1)
+
+    def p_slot(i):
+        d, chunk = 1 + i // 2, i % 2
+        for way in range(2):
+            src = origin(way, d)
+            p_copy(way, src, d, chunk).wait_recv()
+
+            @pl.when(d + 1 + (chunk + way) % 2 <= half_ring)
+            def _():
+                p_copy(way, src, d + 1, chunk).start()
+
+    def use_p(j):
+        use_passages(origin(j % 2, 1 + j // 2))
+
     use_passages(r)
-
-    def p_step(d, carry):
-        for chunk in range(2):
-            for way in range(2):
-                src = origin(way, d)
-                p_copy(way, src, d, chunk).wait_recv()
-                if chunk == way:
-                    p_copy(way, src, d + 1, chunk).start()
-                else:
-                    @pl.when(d + 1 < half_ring)
-                    def _():
-                        p_copy(way, src, d + 1, chunk).start()
-
-        @pl.when(d + 1 == half_ring)
-        def _():
-            for chunk in range(2):
-                for way in range(2):
-                    q_copy(way, r, 1, chunk).start()
-
+    p_slot(0)
+    p_slot(1)
+
+    def p_step(i, carry):
+        p_slot(i)
+        use_p(i - 2)
+        return carry
+
+    lax.fori_loop(2, slots, p_step, 0)
+    for chunk in range(2):
         for way in range(2):
-            use_passages(origin(way, d))
-        return carry
-
-    lax.fori_loop(1, half_ring, p_step, 0)
+            q_copy(way, r, 1, chunk).start()
+    use_p(slots - 2)
+    use_p(slots - 1)
     last = origin(0, half_ring)
     for way in range(2):
         p_copy(way, last, half_ring, way).wait_recv()
     use_passages(last)
 
+    def q_slot(i):
+        d, chunk = 1 + i // 2, i % 2
+        for way in range(2):
+            src = origin(way, d)
+            q_copy(way, src, d, chunk).wait_recv()
+
+            @pl.when(d + 1 + (chunk + way) % 2 <= half_ring)
+            def _():
+                q_copy(way, src, d + 1, chunk).start()
+
+            f_copy(way, src, d, chunk, core).start()
+
+    early = min(3, slots)
+
+    def q_early(i):
+        if i < early:
+            q_slot(i)
+
     lane = lax.broadcasted_iota(jnp.int32, (Rq, 128), 1)
     cols = jnp.where(lane == 0, m_ref[...], jnp.where(lane == 1, l_ref[...], c_ref[...]))
     stats[...] = cols.T[0:8, :]
@@ -174,6 +199,7 @@
 
     for k in range(1, G):
         st_copy(k, g).start()
+    q_early(0)
     for k in range(1, G):
         st_copy(k, (g - k + G) % G).wait_recv()
     stats_in[g] = stats[...]
@@ -200,6 +226,7 @@
     other = pl.ds(pl.multiple_of((1 - core) * hr, hr), hr)
     core_copy = remote(acc.at[other], got_core, x_send.at[0], x_recv.at[0], to_grp(partner))
     core_copy.start()
+    q_early(1)
     core_copy.wait_recv()
     half_sum[...] = acc[mine] + got_core[...]
 
@@ -210,45 +237,44 @@
     for k in range(1, G // 2):
         y_copy(k).start()
 
+    q_early(2)
+
     gp_ref[...] = jnp.zeros((Pd, D), F32)
     base = (r * G + g) * Pd
 
     def use_queries(u):
         block = q_all.at[u]
-        s_keep[u] = dot_nt(p_all[r], block[...])
+        s = dot_nt(p_all[r], block[...])
+        w = jnp.exp(s - lse_all[u][0:1]).astype(BF16)
         row = base + lax.broadcasted_iota(jnp.int32, (Pd, Rq), 0)
         one = jnp.where(row == pos_all[u][0:1], 1.0, 0.0).astype(BF16)
         for t in range(0, D, tile):
             c = pl.ds(t, tile)
-            gp_ref[:, c] -= dot_nn(one, block[:, c])
+            gp_ref[:, c] += dot_nn(w, block[:, c]) - dot_nn(one, block[:, c])
+
+    def use_q(j):
+        d, way = 1 + j // 2, j % 2
+        src = origin(way, d)
+        for chunk in range(2):
+            f_copy(way, src, d, chunk, 1 - core).wait_recv()
+        use_queries(src)
 
     for k in range(1, R):
         pos_copy(k, (r - k + R) % R).wait_recv()
+        lse_copy(k, (r - k + R) % R).wait_recv()
     use_queries(r)
 
-    def q_step(d, carry):
-        for chunk in range(2):
-            for way in range(2):
-                src = origin(way, d)
-                q_copy(way, src, d, chunk).wait_recv()
-                if chunk == way:
-                    q_copy(way, src, d + 1, chunk).start()
-                else:
-                    @pl.when(d + 1 < half_ring)
-                    def _():
-                        q_copy(way, src, d + 1, chunk).start()
-                f_copy(way, src, d, chunk, core).start()
-        for way in range(2):
-            src = origin(way, d)
-            for chunk in range(2):
-                f_copy(way, src, d, chunk, 1 - core).wait_recv()
-            use_queries(src)
+    def q_step(i, carry):
+        q_slot(i)
+        use_q(i - early)
         return carry
 
-    lax.fori_loop(1, half_ring, q_step, 0)
+    lax.fori_loop(early, slots, q_step, 0)
+    use_q(slots - early)
     for way in range(2):
         q_copy(way, last, half_ring, way).wait_recv()
         f_copy(way, last, half_ring, way, core).start()
+    lax.fori_loop(slots - early + 1, slots - 1, lambda j, c: (use_q(j), c)[1], 0)
 
     for k in range(1, G // 2):
         y_copy(k).wait_recv()
@@ -260,27 +286,11 @@
     back_copy.start()
     gq_ref[mine] = whole
 
+    if early > 1:
+        use_q(slots - 1)
     for way in range(2):
         f_copy(way, last, half_ring, way, 1 - core).wait_recv()
     use_queries(last)
-    for k in range(1, R):
-        lse_copy(k, (r - k + R) % R).wait_recv()
-
-    def weigh(u, carry):
-        at = pl.ds(pl.multiple_of(u * Rq, Rq), Rq)
-        w_keep[:, at] = jnp.exp(s_keep[u] - lse_all[u][0:1]).astype(BF16)
-        return carry
-
-    lax.fori_loop(0, R, weigh, 0)
-
-    def passages_tile(t, carry):
-        c = pl.ds(pl.multiple_of(t * tile, tile), tile)
-        q_cols = q_all[:, :, c].reshape(R * Rq, tile)
-        gp_ref[:, c] += dot_nn(w_keep[...], q_cols)
-        return carry
-
-    lax.fori_loop(0, D // tile, passages_tile, 0)
-
     back_copy.wait_recv()
     gq_ref[other] = got_half[...]
 
@@ -315,8 +325,6 @@
 def local(R, G, queries, passages, positive):
     Rq, D = queries.shape
     Pd = passages.shape[0]
-    pos_col = positive[:, None]
-    pos_row = jnp.broadcast_to(positive[None, :], (8, Rq))
     ring = (2, R // 2 + 1, 2)
     sem = pltpu.SemaphoreType.DMA
     vmem = pltpu.VMEM
@@ -330,7 +338,6 @@
         in_specs=[
             pl.BlockSpec(memory_space=pl.ANY),
             pl.BlockSpec(memory_space=pl.ANY),
-            pl.BlockSpec(memory_space=vmem),
             pl.BlockSpec(memory_space=vmem),
         ],
         out_specs=[pl.BlockSpec(memory_space=vmem)] * 3,
@@ -347,8 +354,8 @@
             vmem((Rq, 1), F32),
             vmem((Rq, 1), F32),
             vmem((Rq, 1), F32),
-            vmem((R, Pd, Rq), F32),
-            vmem((Pd, R * Rq), BF16),
+            vmem((Rq, 1), jnp.int32),
+            vmem((8, Rq), jnp.int32),
             vmem((Rq // 2, D), F32),
             vmem((Rq // 2, D), F32),
             vmem((G // 2 - 1, Rq // 2, D), F32),
@@ -360,10 +367,10 @@
             sem((2,)), sem((2,)), sem((G // 2,)), sem((G // 2,)),
         ],
         compiler_params=pltpu.CompilerParams(
-            collective_id=0, has_side_effects=True, vmem_limit_bytes=60 * 1024 * 1024
+            collective_id=0, has_side_effects=True, vmem_limit_bytes=min(R * (Pd + Rq) * D * 2 + 16 * Rq * D * 4, 60 * 1024 * 1024)
         ),
         name="infonce",
-    )(queries, passages, pos_col, pos_row)
+    )(queries, passages, positive[None, :])
     return losses[0], gq, gp
 
 

time: 91.2 us -> 82.7 us (0.907)
  Pallas kernels: 82.9 us -> 76.6 us
  local copies, waits for them, and re-layouts: 6.65 us -> 5.26 us
    pallas_call x1, Pallas kernels: 82.9 us -> 76.6 us  [local(): pl.pallas_call(functools.partial(kernel, R, G), out_shape=(jax.ShapeDtype...]
    broadcast_in_dim x2 -> x0, local copies, waits for them, and re-layouts: 1.4 us -> none  [the longest x1 0.8 us: local(): pos_col = positive[:, None]]
where the time goes in v2:
time: 82.7 us; the launch traced here: 82.5 us
  Pallas kernels  76.6 us (93%)
  local copies, waits for them, and re-layouts  5.26 us (6%)
    pallas_call x1, Pallas kernels, local(): pl.pallas_call(functools.partial(kernel, R, G), out_shape=(jax.ShapeDtype...  76.6 us
    unnamed x9, local copies, waits for them, and re-layouts  5.26 us

profile of v2, /device:TPU:0, one launch (start us, length us, event | category | flops | bytes accessed | tf_op | source)
XLA Modules:
  0.0 82.5 jit_solution(14128147398862772508)
XLA Ops:
  0.6 0.0 copy-start.2
  0.6 0.7 copy-done.2
  1.3 0.0 copy-start
  1.3 1.0 %copy-done = bf16[256,1024]{1,0:T(8,128)(2,1)S(1)} copy-done((bf16[256,1024]{1,0:T(8,128)(2,1)S(1)}, bf16[256,1024]{1,0:T(8,128)(2,1)}, u32[]{:S(2)}) %copy-start) | copy-done | bytes 524312
  2.4 0.0 copy-start.1
  2.4 1.0 %copy-done.1 = bf16[256,1024]{1,0:T(8,128)(2,1)S(1)} copy-done((bf16[256,1024]{1,0:T(8,128)(2,1)S(1)}, bf16[256,1024]{1,0:T(8,128)(2,1)}, u32[]{:S(2)}) %copy-start.1) | copy-done | bytes 524312
  3.4 76.6 %infonce.1 = (f32[1,256]{1,0:T(1,128)S(1)}, f32[256,1024]{1,0:T(8,128)S(1)}, f32[256,1024]{1,0:T(8,128)S(1)}) custom-call(bf16[256,1024]{1,0:T(8,128)(2,1)S(1)} %copy-done, bf16[256,1024]{1,0:T(8,128)(2,1)S(1)} %copy-done.1, s32[1,256]{1,0:T(1,128)S(1)} %bitcast.2), custom_call_target="tpu_custom_call" | custom-call | tf_op jit(solution)/shard_map/infonce/pallas_call | solution.py:331
  80.0 0.6 copy.9
  80.5 1.0 %copy.10 = f32[256,1024]{1,0:T(8,128)} copy(f32[256,1024]{1,0:T(8,128)S(1)} %get-tuple-element.13) | data formatting | bytes 2097152
  81.5 1.0 %copy.11 = f32[256,1024]{1,0:T(8,128)} copy(f32[256,1024]{1,0:T(8,128)S(1)} %get-tuple-element.14) | data formatting | bytes 2097152
Async XLA Ops:
  0.6 0.7 copy-start.2
  1.3 1.0 %copy-start = (bf16[256,1024]{1,0:T(8,128)(2,1)S(1)}, bf16[256,1024]{1,0:T(8,128)(2,1)}, u32[]{:S(2)}) copy-start(bf16[256,1024]{1,0:T(8,128)(2,1)} %q_hbm.1) | copy-start | bytes 1572868
  2.4 1.0 %copy-start.1 = (bf16[256,1024]{1,0:T(8,128)(2,1)S(1)}, bf16[256,1024]{1,0:T(8,128)(2,1)}, u32[]{:S(2)}) copy-start(bf16[256,1024]{1,0:T(8,128)(2,1)} %p_hbm.1) | copy-start | bytes 1572868

commit v3 on v2

--- a/solution.py
+++ b/solution.py
@@ -25,7 +25,7 @@
     R, G, q_hbm, p_hbm, pos_ref,
     loss_ref, gq_ref, gp_ref,
     p_all, q_all, pos_all, lse_all, stats, stats_in, lse_buf,
-    acc, hit_acc, m_ref, l_ref, c_ref, pos_col_ref, pos_row_ref,
+    acc, hit_acc, m_ref, l_ref, c_ref, final_ref, pos_col_ref, pos_row_ref,
     got_core, half_sum, got_y, done_half, got_half,
     local_sem, p_send, p_recv, q_send, q_recv, f_send, f_recv,
     pos_send, pos_recv, lse_send, lse_recv, st_send, st_recv,
@@ -117,7 +117,7 @@
     acc[...] = jnp.zeros((Rq, D), F32)
     hit_acc[...] = jnp.zeros((Rq, D), F32)
 
-    def use_passages(u):
+    def use_passages(u, between=None):
         block = p_all.at[u]
         s = dot_nt(q_all[r], block[...])
         column = (u * G + g) * Pd + lax.broadcasted_iota(jnp.int32, (Rq, Pd), 1)
@@ -129,6 +129,8 @@
         w = jnp.exp(s - new)
         l_ref[...] = l_ref[...] * scale + jnp.sum(w, axis=1, keepdims=True)
         m_ref[...] = new
+        if between is not None:
+            between()
         w = w.astype(BF16)
         one = jnp.where(hit, 1.0, 0.0).astype(BF16)
         for t in range(0, D, tile):
@@ -169,7 +171,19 @@
     last = origin(0, half_ring)
     for way in range(2):
         p_copy(way, last, half_ring, way).wait_recv()
-    use_passages(last)
+
+    def st_copy(k, src):
+        return remote(stats, stats_in.at[src], st_send.at[k], st_recv.at[k],
+                      to_grp((g + k) % G))
+
+    def send_stats():
+        lane = lax.broadcasted_iota(jnp.int32, (Rq, 128), 1)
+        cols = jnp.where(lane == 0, m_ref[...], jnp.where(lane == 1, l_ref[...], c_ref[...]))
+        stats[...] = cols.T[0:8, :]
+        for k in range(1, G):
+            st_copy(k, g).start()
+
+    use_passages(last, send_stats)
 
     def q_slot(i):
         d, chunk = 1 + i // 2, i % 2
@@ -189,17 +203,6 @@
         if i < early:
             q_slot(i)
 
-    lane = lax.broadcasted_iota(jnp.int32, (Rq, 128), 1)
-    cols = jnp.where(lane == 0, m_ref[...], jnp.where(lane == 1, l_ref[...], c_ref[...]))
-    stats[...] = cols.T[0:8, :]
-
-    def st_copy(k, src):
-        return remote(stats, stats_in.at[src], st_send.at[k], st_recv.at[k],
-                      to_grp((g + k) % G))
-
-    for k in range(1, G):
-        st_copy(k, g).start()
-    q_early(0)
     for k in range(1, G):
         st_copy(k, (g - k + G) % G).wait_recv()
     stats_in[g] = stats[...]
@@ -220,24 +223,49 @@
 
     lse_col = jnp.broadcast_to(lse, (128, Rq)).T[:, 0:1]
     hr = Rq // 2
-    final = jnp.exp(m_ref[...] - lse_col)
-    acc[...] = acc[...] * final - hit_acc[...]
-    mine = pl.ds(pl.multiple_of(core * hr, hr), hr)
-    other = pl.ds(pl.multiple_of((1 - core) * hr, hr), hr)
-    core_copy = remote(acc.at[other], got_core, x_send.at[0], x_recv.at[0], to_grp(partner))
-    core_copy.start()
+    final_ref[...] = jnp.exp(m_ref[...] - lse_col)
+    pieces = got_core.shape[0]
+    pr = hr // pieces
+
+    def piece_of(whose, n):
+        return pl.ds(pl.multiple_of(whose * hr + n * pr, pr), pr)
+
+    def core_copy(n):
+        return remote(acc.at[piece_of(1 - core, n)], got_core.at[n],
+                      x_send.at[0, n], x_recv.at[0, n], to_grp(partner))
+
+    def y_copy(k, n):
+        return remote(half_sum.at[n], got_y.at[k - 1, n], y_send.at[k, n], y_recv.at[k, n],
+                      to_grp((g + 2 * k) % G))
+
+    def back_copy(n):
+        return remote(done_half.at[n], got_half.at[n], x_send.at[1, n], x_recv.at[1, n],
+                      to_grp(partner))
+
+    for n in range(pieces):
+        at = piece_of(1 - core, n)
+        acc[at] = acc[at] * final_ref[at] - hit_acc[at]
+        core_copy(n).start()
+    for n in range(pieces):
+        at = piece_of(core, n)
+        acc[at] = acc[at] * final_ref[at] - hit_acc[at]
+    q_early(0)
+    for n in range(pieces):
+        core_copy(n).wait_recv()
+        half_sum[n] = acc[piece_of(core, n)] + got_core[n]
+        for k in range(1, G // 2):
+            y_copy(k, n).start()
     q_early(1)
-    core_copy.wait_recv()
-    half_sum[...] = acc[mine] + got_core[...]
-
-    def y_copy(k):
-        return remote(half_sum, got_y.at[k - 1], y_send.at[k], y_recv.at[k],
-                      to_grp((g + 2 * k) % G))
-
-    for k in range(1, G // 2):
-        y_copy(k).start()
-
     q_early(2)
+
+    def finish_piece(n):
+        whole = half_sum[n]
+        for k in range(1, G // 2):
+            y_copy(k, n).wait_recv()
+            whole = whole + got_y[k - 1, n]
+        done_half[n] = whole
+        back_copy(n).start()
+        gq_ref[piece_of(core, n)] = whole
 
     gp_ref[...] = jnp.zeros((Pd, D), F32)
     base = (r * G + g) * Pd
@@ -269,30 +297,24 @@
         use_q(i - early)
         return carry
 
-    lax.fori_loop(early, slots, q_step, 0)
+    unrolled = min(early + pieces - 1, slots)
+    for i in range(early, unrolled):
+        q_step(i, 0)
+        finish_piece(i - early)
+    lax.fori_loop(unrolled, slots, q_step, 0)
     use_q(slots - early)
     for way in range(2):
         q_copy(way, last, half_ring, way).wait_recv()
         f_copy(way, last, half_ring, way, core).start()
-    lax.fori_loop(slots - early + 1, slots - 1, lambda j, c: (use_q(j), c)[1], 0)
-
-    for k in range(1, G // 2):
-        y_copy(k).wait_recv()
-    whole = half_sum[...]
-    for k in range(1, G // 2):
-        whole = whole + got_y[k - 1]
-    done_half[...] = whole
-    back_copy = remote(done_half, got_half, x_send.at[1], x_recv.at[1], to_grp(partner))
-    back_copy.start()
-    gq_ref[mine] = whole
-
-    if early > 1:
-        use_q(slots - 1)
+    for n in range(unrolled - early, pieces):
+        finish_piece(n)
+    lax.fori_loop(slots - early + 1, slots, lambda j, c: (use_q(j), c)[1], 0)
     for way in range(2):
         f_copy(way, last, half_ring, way, 1 - core).wait_recv()
     use_queries(last)
-    back_copy.wait_recv()
-    gq_ref[other] = got_half[...]
+    for n in range(pieces):
+        back_copy(n).wait_recv()
+        gq_ref[piece_of(1 - core, n)] = got_half[n]
 
     def drain(d, carry):
         for chunk in range(2):
@@ -316,16 +338,19 @@
         lse_copy(k, r).wait_send()
     for k in range(1, G):
         st_copy(k, g).wait_send()
-    for k in range(1, G // 2):
-        y_copy(k).wait_send()
-    core_copy.wait_send()
-    back_copy.wait_send()
+    for n in range(pieces):
+        for k in range(1, G // 2):
+            y_copy(k, n).wait_send()
+        core_copy(n).wait_send()
+        back_copy(n).wait_send()
 
 
 def local(R, G, queries, passages, positive):
     Rq, D = queries.shape
     Pd = passages.shape[0]
     ring = (2, R // 2 + 1, 2)
+    pieces = 4
+    pr = Rq // 2 // pieces
     sem = pltpu.SemaphoreType.DMA
     vmem = pltpu.VMEM
     losses, gq, gp = pl.pallas_call(
@@ -336,8 +361,8 @@
             jax.ShapeDtypeStruct((Pd, D), F32),
         ),
         in_specs=[
-            pl.BlockSpec(memory_space=pl.ANY),
-            pl.BlockSpec(memory_space=pl.ANY),
+            pl.BlockSpec(memory_space=pltpu.HBM),
+            pl.BlockSpec(memory_space=pltpu.HBM),
             pl.BlockSpec(memory_space=vmem),
         ],
         out_specs=[pl.BlockSpec(memory_space=vmem)] * 3,
@@ -354,17 +379,18 @@
             vmem((Rq, 1), F32),
             vmem((Rq, 1), F32),
             vmem((Rq, 1), F32),
+            vmem((Rq, 1), F32),
             vmem((Rq, 1), jnp.int32),
             vmem((8, Rq), jnp.int32),
-            vmem((Rq // 2, D), F32),
-            vmem((Rq // 2, D), F32),
-            vmem((G // 2 - 1, Rq // 2, D), F32),
-            vmem((Rq // 2, D), F32),
-            vmem((Rq // 2, D), F32),
+            vmem((pieces, pr, D), F32),
+            vmem((pieces, pr, D), F32),
+            vmem((G // 2 - 1, pieces, pr, D), F32),
+            vmem((pieces, pr, D), F32),
+            vmem((pieces, pr, D), F32),
             sem((2,)),
             sem(ring), sem(ring), sem(ring), sem(ring), sem(ring), sem(ring),
             sem((R,)), sem((R,)), sem((R,)), sem((R,)), sem((G,)), sem((G,)),
-            sem((2,)), sem((2,)), sem((G // 2,)), sem((G // 2,)),
+            sem((2, pieces)), sem((2, pieces)), sem((G // 2, pieces)), sem((G // 2, pieces)),
         ],
         compiler_params=pltpu.CompilerParams(
             collective_id=0, has_side_effects=True, vmem_limit_bytes=min(R * (Pd + Rq) * D * 2 + 16 * Rq * D * 4, 60 * 1024 * 1024)

time: 82.7 us -> 85.4 us (1.033)
  Pallas kernels: 76.6 us -> 79.3 us
    pallas_call x1, Pallas kernels: 76.6 us -> 79.3 us  [local(): pl.pallas_call(functools.partial(kernel, R, G), out_shape=(jax.ShapeDtype...]
where the time goes in v3:
time: 85.4 us; the launch traced here: 85.2 us
  Pallas kernels  79.3 us (93%)
  local copies, waits for them, and re-layouts  5.26 us (6%)
    pallas_call x1, Pallas kernels, local(): pl.pallas_call(functools.partial(kernel, R, G), out_shape=(jax.ShapeDtype...  79.3 us
    unnamed x9, local copies, waits for them, and re-layouts  5.26 us

profile of v3, /device:TPU:0, one launch (start us, length us, event | category | flops | bytes accessed | tf_op | source)
XLA Modules:
  0.0 85.2 jit_solution(11881522851245173437)
XLA Ops:
  0.6 0.0 copy-start.2
  0.6 0.7 copy-done.2
  1.3 0.0 copy-start
  1.3 1.0 %copy-done = bf16[256,1024]{1,0:T(8,128)(2,1)S(1)} copy-done((bf16[256,1024]{1,0:T(8,128)(2,1)S(1)}, bf16[256,1024]{1,0:T(8,128)(2,1)}, u32[]{:S(2)}) %copy-start) | copy-done | bytes 524312
  2.4 0.0 copy-start.1
  2.4 1.0 %copy-done.1 = bf16[256,1024]{1,0:T(8,128)(2,1)S(1)} copy-done((bf16[256,1024]{1,0:T(8,128)(2,1)S(1)}, bf16[256,1024]{1,0:T(8,128)(2,1)}, u32[]{:S(2)}) %copy-start.1) | copy-done | bytes 524312
  3.4 79.3 %infonce.1 = (f32[1,256]{1,0:T(1,128)S(1)}, f32[256,1024]{1,0:T(8,128)S(1)}, f32[256,1024]{1,0:T(8,128)S(1)}) custom-call(bf16[256,1024]{1,0:T(8,128)(2,1)S(1)} %copy-done, bf16[256,1024]{1,0:T(8,128)(2,1)S(1)} %copy-done.1, s32[1,256]{1,0:T(1,128)S(1)} %bitcast.2), custom_call_target="tpu_custom_call" | custom-call | tf_op jit(solution)/shard_map/infonce/pallas_call | solution.py:356
  82.7 0.6 copy.9
  83.2 1.0 %copy.10 = f32[256,1024]{1,0:T(8,128)} copy(f32[256,1024]{1,0:T(8,128)S(1)} %get-tuple-element.13) | data formatting | bytes 2097152
  84.2 1.0 %copy.11 = f32[256,1024]{1,0:T(8,128)} copy(f32[256,1024]{1,0:T(8,128)S(1)} %get-tuple-element.14) | data formatting | bytes 2097152
Async XLA Ops:
  0.6 0.7 copy-start.2
  1.3 1.0 %copy-start = (bf16[256,1024]{1,0:T(8,128)(2,1)S(1)}, bf16[256,1024]{1,0:T(8,128)(2,1)}, u32[]{:S(2)}) copy-start(bf16[256,1024]{1,0:T(8,128)(2,1)} %q_hbm.1) | copy-start | bytes 1572868
  2.4 1.0 %copy-start.1 = (bf16[256,1024]{1,0:T(8,128)(2,1)S(1)}, bf16[256,1024]{1,0:T(8,128)(2,1)}, u32[]{:S(2)}) copy-start(bf16[256,1024]{1,0:T(8,128)(2,1)} %p_hbm.1) | copy-start | bytes 1572868
